TPU v7x, 32 devices: a whole 2x2x4 slice. The times are simulated.
32 devices in a mesh: section: 2 (over core), dp: 8 (over z, x), tensor: 2 (over y).
Axes of the slice: x: 2, y: 2, z: 4, core: 2. Of those that a mesh axis runs over, the one named last changes fastest.
Arguments:
- tokens: bfloat16 [1024, 4096], P('dp', 'tensor'), may hold values from -6 to 6
- gain: bfloat16 [2, 4096], P('section', 'tensor'), may hold values from 0.099609375 to 1.8984375
- w_up: bfloat16 [2, 4096, 5120], P('section', 'dp', 'tensor'), may hold values from -0.09375 to 0.09375
- w_down: bfloat16 [2, 5120, 4096], P('section', 'tensor', 'dp'), may hold values from -0.078125 to 0.078125
- cotangent: bfloat16 [2, 1024, 4096], P('section', 'dp'), may hold values from -6 to 6
Outputs:
- states: bfloat16 [2, 1024, 4096], P('section', 'dp', 'tensor')
- grad_down: bfloat16 [2, 5120, 4096], P('section', 'tensor', 'dp')
All inputs are finite; a program needn't handle non-finite values.
Results may differ from a plain program's by a relative error of at most 0.02.
Values may be sent and summed in bfloat16 or wider, within the bound.
A program may use at most 128 MiB of HBM per device.

v0:
```python
import jax
import jax.numpy as jnp
from jax import lax
from jax.sharding import PartitionSpec as P

EPS = 1e-06
F32 = jnp.float32
BF16 = jnp.bfloat16


def body(tokens, gain, w_up, w_down, cotangent):
    core = lax.axis_index("section")
    layers = lax.axis_size("section")
    assert layers == 2
    dp_id = lax.axis_index("dp")
    dp_count = lax.axis_size("dp")
    tensor_id = lax.axis_index("tensor")
    tensor_count = lax.axis_size("tensor")
    rows, own_width = tokens.shape
    width = own_width * tensor_count
    slice_width = width // dp_count
    hidden_width = w_up.shape[2]
    half = hidden_width // layers
    other = 1 - core
    all_rows = rows * dp_count

    def swap(array):
        return lax.ppermute(array, "section", [(0, 1), (1, 0)])

    def both(own, got):
        return (jnp.where(core == 0, own, got), jnp.where(core == 0, got, own))

    cot_mine = lax.all_to_all(cotangent[0], "dp", split_axis=1, concat_axis=0, tiled=True)
    half_rows = rows // layers
    tok_half = lax.dynamic_slice_in_dim(tokens, core * half_rows, half_rows, 0)
    tok_full = lax.all_gather(tok_half, "tensor", axis=1, tiled=True)
    tok_f = tok_full.astype(F32)
    sums_half = jnp.sum(tok_f * tok_f, axis=1)
    sums_a, sums_b = both(sums_half, swap(sums_half))
    sums = jnp.concatenate([sums_a, sums_b])
    x_half = lax.all_to_all(tok_full, "dp", split_axis=1, concat_axis=0, tiled=True)
    x_a, x_b = both(x_half, swap(x_half))
    x = jnp.concatenate(
        [
            x_a.reshape(dp_count, half_rows, slice_width),
            x_b.reshape(dp_count, half_rows, slice_width),
        ],
        axis=1,
    ).reshape(all_rows, slice_width)
    gain_all = lax.all_gather(gain, "tensor", axis=1, tiled=True)
    gain_own = lax.dynamic_slice_in_dim(gain_all, dp_id * slice_width, slice_width, 1)
    gains = both(gain_own, swap(gain_own))
    up_parts = both(
        lax.dynamic_slice_in_dim(w_up[0], core * half, half, 1),
        swap(lax.dynamic_slice_in_dim(w_up[0], other * half, half, 1)),
    )
    down_parts = both(
        lax.dynamic_slice_in_dim(w_down[0], core * half, half, 0),
        swap(lax.dynamic_slice_in_dim(w_down[0], other * half, half, 0)),
    )
    states = []
    hiddens = []
    for layer in range(layers):
        x_f = x.astype(F32)
        if layer > 0:
            sums = lax.psum_scatter(
                jnp.sum(x_f * x_f, axis=1), "dp", scatter_dimension=0, tiled=True
            )
        scaled = (x_f * gains[layer].astype(F32)).astype(BF16)
        part = jnp.dot(scaled, up_parts[layer], preferred_element_type=F32).astype(BF16)
        pre = lax.psum_scatter(part, "dp", scatter_dimension=0, tiled=True)
        inverse_rms = lax.rsqrt(sums / width + EPS)
        hidden = jax.nn.gelu(pre.astype(F32) * inverse_rms[:, None], approximate=True).astype(BF16)
        hidden_all = lax.all_gather(hidden, "dp", axis=0, tiled=True)
        hiddens.append(hidden_all)
        out = jnp.dot(hidden_all, down_parts[layer], preferred_element_type=F32)
        mid = all_rows // layers
        keep = lax.dynamic_slice_in_dim(out, core * mid, mid, 0)
        give = lax.dynamic_slice_in_dim(out, other * mid, mid, 0).astype(BF16)
        summed = keep + swap(give).astype(F32)
        if tensor_count == 2:
            sent = summed.astype(BF16)
            got = lax.ppermute(sent, "tensor", [(0, 1), (1, 0)])
            summed = sent.astype(F32) + got.astype(F32)
        else:
            summed = lax.psum(summed.astype(BF16), "tensor").astype(F32)
        x_mid = lax.dynamic_slice_in_dim(x_f, core * mid, mid, 0)
        new_mid = (x_mid + summed).astype(BF16)
        new_a, new_b = both(new_mid, swap(new_mid))
        x = jnp.concatenate([new_a, new_b], axis=0)
        states.append(x)
    state_own = jnp.where(core == 0, states[0], states[1])
    state_rows = lax.all_to_all(state_own, "dp", split_axis=0, concat_axis=1, tiled=True)
    state = lax.dynamic_slice_in_dim(state_rows, tensor_id * own_width, own_width, 1)
    hid_keep = jnp.where(core == 0, hiddens[0], hiddens[1])
    hid_got = swap(jnp.where(core == 0, hiddens[1], hiddens[0]))
    hid_parts = both(hid_keep, hid_got)
    hidden_whole = jnp.concatenate(hid_parts, axis=1)
    grad = lax.dot_general(
        hidden_whole, cot_mine, (((0,), (0,)), ((), ())), preferred_element_type=F32
    ).astype(BF16)
    return (state[None], grad[None])


def solution(mesh):
    placed = (
        P("dp", "tensor"),
        P("section", "tensor"),
        P("section", "dp", "tensor"),
        P("section", "tensor", "dp"),
        P("section", "dp", None),
    )
    return jax.shard_map(
        body,
        mesh=mesh,
        in_specs=placed,
        out_specs=(P("section", "dp", "tensor"), P("section", "tensor", "dp")),
        check_vma=False,
    )
```

profile of v0, /device:TPU:0, one launch (start us, length us, event | category | flops | bytes accessed | tf_op | source)
XLA Modules:
  0.0 413.5 jit_solution(5616129061812105178)
XLA Ops:
  8.2 10.0 %all_gather.12 = bf16[64,4096]{1,0:T(8,128)(2,1)S(1)} all-gather(bf16[64,2048]{1,0:T(8,128)(2,1)S(1)} %constant_dynamic-slice_fusion.2), channel_id=1, replica_groups=mesh['section'=2,'dp'=8,'tensor'=2] {'tensor'}, dimensions={1}, use_global_device_ids=true | all-gather | bytes 786432 | tf_op jit(solution)/shard_map/all_gather | solution.py:36
  19.0 6.2 %all-to-all-start = ((bf16[64,8,512]{2,0,1:T(8,128)(2,1)}), bf16[64,8,512]{2,0,1:T(8,128)(2,1)S(1)}, u32[]{:S(2)}, u32[]{:S(2)}) async-start(bf16[64,8,512]{2,0,1:T(8,128)(2,1)} %bitcast.43), calls=%async_computation | async-start | bytes 1048576 | tf_op jit(solution)/shard_map/all_to_all | solution.py:41
  25.3 2.5 dynamic-slice_bitcast_fusion.1
  27.7 11.2 %all-to-all-done = bf16[64,8,512]{2,0,1:T(8,128)(2,1)S(1)} async-done(((bf16[64,8,512]{2,0,1:T(8,128)(2,1)}), bf16[64,8,512]{2,0,1:T(8,128)(2,1)S(1)}, u32[]{:S(2)}, u32[]{:S(2)}) %all-to-all-start) | async-done | bytes 524320 | tf_op jit(solution)/shard_map/all_to_all | solution.py:41
  38.9 4.3 %all_gather.13 = bf16[1,4096]{1,0:T(2,128)(2,1)S(1)} all-gather(bf16[1,2048]{1,0:T(2,128)(2,1)S(1)} %copy-done.12), channel_id=1, replica_groups=mesh['section'=2,'dp'=8,'tensor'=2] {'tensor'}, dimensions={1}, use_global_device_ids=true | all-gather | bytes 12288 | tf_op jit(solution)/shard_map/all_gather | solution.py:50
  46.4 3.1 convolution_convert_fusion.1
  52.2 68.8 %reduce-scatter.3.cloned.1.call-done = bf16[128,1280]{1,0:T(8,128)(2,1)} async-done(((bf16[1024,1280]{1,0:T(8,128)(2,1)}), bf16[128,1280]{1,0:T(8,128)(2,1)}) %reduce-scatter.3.cloned.1.call-update) | async-done | bytes 327696 | tf_op jit(solution)/shard_map/reduce_scatter | solution.py:71
  123.0 2.5 dynamic-slice_bitcast_fusion
  125.5 3.4 collective-permute-done.4
  128.9 48.4 %all-gather.3.cloned.1.call-done = bf16[1024,1280]{1,0:T(8,128)(2,1)} async-done(((bf16[128,1280]{1,0:T(8,128)(2,1)}), bf16[1024,1280]{1,0:T(8,128)(2,1)}) %all-gather.3.cloned.1.call-update) | async-done | bytes 2621456 | tf_op jit(solution)/shard_map/all_gather | solution.py:74
  177.3 3.7 fusion.10
  188.2 12.5 %collective-permute-done.6 = bf16[512,512]{1,0:T(8,128)(2,1)S(1)} collective-permute-done((bf16[512,512]{1,0:T(8,128)(2,1)S(1)}, bf16[512,512]{1,0:T(8,128)(2,1)S(1)}, u32[]{:S(2)}, u32[]{:S(2)}) %collective-permute-start.6) | collective-permute-done | bytes 524320 | tf_op jit(solution)/shard_map/ppermute | solution.py:83
  203.0 4.8 %convolution_convert_fusion = bf16[1024,1280]{1,0:T(8,128)(2,1)} fusion(bf16[512,1280]{1,0:T(8,128)(2,1)} %collective-permute-done.2, pred[]{:T(512)S(6)} %eq.2, bf16[1,512,2560]{2,1,0:T(8,128)(2,1)S(1)} %copy-done.11, s32[]{:T(128)S(6)} %select_n.145, f32[512]{0:T(512)S(1)} %bitcast.52, bf16[512,512]{1,0:T(8,128)(2,1)S(1)} %get-tuple-element.7, ...), kind=kOutput, calls=%fused_computation.6 | convolution fusion | flops 1347289088 | bytes 6293509 | tf_op jit(solution)/shard_map/dot_general | solution.py:70
  209.9 19.5 %all-reduce = f32[1024]{0:T(1024)S(1)} all-reduce(f32[1024]{0:T(1024)S(1)} %multiply_reduce_fusion), channel_id=4, replica_groups=mesh['section'=2,'dp'=8,'tensor'=2] {'dp'}, use_global_device_ids=true, to_apply=%region_4.5.clone | all-reduce | flops 1024 | bytes 8192
  229.5 48.0 %reduce-scatter.5.cloned.1.call-done = bf16[128,1280]{1,0:T(8,128)(2,1)} async-done(((bf16[1024,1280]{1,0:T(8,128)(2,1)}), bf16[128,1280]{1,0:T(8,128)(2,1)}) %reduce-scatter.5.cloned.1.call-update) | async-done | bytes 327696 | tf_op jit(solution)/shard_map/reduce_scatter | solution.py:71
  279.5 54.1 %all-gather.5.cloned.1.call-done = bf16[1024,1280]{1,0:T(8,128)(2,1)} async-done(((bf16[128,1280]{1,0:T(8,128)(2,1)}), bf16[1024,1280]{1,0:T(8,128)(2,1)}) %all-gather.5.cloned.1.call-update) | async-done | bytes 2621456 | tf_op jit(solution)/shard_map/all_gather | solution.py:74
  333.7 4.2 %fusion.11 = f32[1024,512]{1,0:T(8,128)S(1)} fusion(bf16[1024,1280]{1,0:T(8,128)(2,1)} %all-gather.5.cloned.1.call-done, bf16[1280,512]{1,0:T(8,128)(2,1)} %collective-permute-done.4, pred[]{:T(512)S(6)} %eq.2, bf16[1,2560,512]{2,1,0:T(8,128)(2,1)} %param.8, s32[]{:T(128)S(6)} %select_n.145), kind=kOutput, calls=%fused_computation.18 | convolution fusion | flops 1342832640 | bytes 7340037 | tf_op jit(solution)/shard_map/dot_general | solution.py:76
  344.7 4.2 %all-to-all-start.2 = ((bf16[128,8,512]{0,2,1:T(8,128)(2,1)}), bf16[128,8,512]{0,2,1:T(8,128)(2,1)}, u32[]{:S(2)}, u32[]{:S(2)}) async-start(bf16[128,8,512]{0,2,1:T(8,128)(2,1)} %bitcast.45), calls=%async_computation.4 | async-start | bytes 2097152 | tf_op jit(solution)/shard_map/all_to_all | solution.py:33
  352.4 12.1 %collective-permute-done.9 = bf16[512,512]{1,0:T(8,128)(2,1)S(1)} collective-permute-done((bf16[512,512]{1,0:T(8,128)(2,1)S(1)}, bf16[512,512]{1,0:T(8,128)(2,1)S(1)}, u32[]{:S(2)}, u32[]{:S(2)}) %collective-permute-start.9) | collective-permute-done | bytes 524320 | tf_op jit(solution)/shard_map/ppermute | solution.py:83
  370.3 4.8 %all-to-all-done.2 = bf16[128,8,512]{0,2,1:T(8,128)(2,1)} async-done(((bf16[128,8,512]{0,2,1:T(8,128)(2,1)}), bf16[128,8,512]{0,2,1:T(8,128)(2,1)}, u32[]{:S(2)}, u32[]{:S(2)}) %all-to-all-start.2) | async-done | bytes 1048608 | tf_op jit(solution)/shard_map/all_to_all | solution.py:33
  375.1 4.4 %all-to-all-start.1 = ((bf16[8,128,512]{1,2,0:T(8,128)(2,1)}), bf16[8,128,512]{1,2,0:T(8,128)(2,1)}, u32[]{:S(2)}, u32[]{:S(2)}) async-start(bf16[8,128,512]{1,2,0:T(8,128)(2,1)} %copy.16), calls=%async_computation.3 | async-start | bytes 2097152 | tf_op jit(solution)/shard_map/all_to_all | solution.py:93
  379.6 2.3 copy.19
  384.1 4.3 %fusion.7 = bf16[1,2560,512]{2,1,0:T(8,128)(2,1)} fusion(bf16[1024,512]{1,0:T(8,128)(2,1)S(1)} %bitcast.50, bf16[1024,1280]{1,0:T(8,128)(2,1)S(1)} %get-tuple-element.3, bf16[1024,1280]{1,0:T(8,128)(2,1)S(1)} %get-tuple-element.2), kind=kOutput, calls=%fused_computation.5 | convolution fusion | flops 2696151040 | bytes 8912896 | tf_op jit(solution)/shard_map/dot_general | solution.py:99
  388.4 16.5 %all-to-all-done.1 = bf16[8,128,512]{1,2,0:T(8,128)(2,1)} async-done(((bf16[8,128,512]{1,2,0:T(8,128)(2,1)}), bf16[8,128,512]{1,2,0:T(8,128)(2,1)}, u32[]{:S(2)}, u32[]{:S(2)}) %all-to-all-start.1) | async-done | bytes 1048608 | tf_op jit(solution)/shard_map/all_to_all | solution.py:93
  (88 shorter events, 43.3 us)
Async XLA Ops:
  19.0 19.8 %copy-start.12 = (bf16[1,2048]{1,0:T(2,128)(2,1)S(1)}, bf16[1,2048]{1,0:T(2,128)(2,1)}, u32[]{:S(2)}) copy-start(bf16[1,2048]{1,0:T(2,128)(2,1)} %param.6) | copy-start | bytes 12292
  19.0 19.8 %all-to-all-start = ((bf16[64,8,512]{2,0,1:T(8,128)(2,1)}), bf16[64,8,512]{2,0,1:T(8,128)(2,1)S(1)}, u32[]{:S(2)}, u32[]{:S(2)}) async-start(bf16[64,8,512]{2,0,1:T(8,128)(2,1)} %bitcast.43), calls=%async_computation | async-start | bytes 1048576 | tf_op jit(solution)/shard_map/all_to_all | solution.py:41
  25.2 95.7 %reduce-scatter.3.cloned.1.call-start = ((), (), s32[]{:S(2)}) async-start(), calls=%async_computation.5 | async-start | bytes 2949120 | tf_op jit(solution)/shard_map/reduce_scatter | solution.py:71
  27.7 17.3 %collective-permute-start.2 = (bf16[512,1280]{1,0:T(8,128)(2,1)}, bf16[512,1280]{1,0:T(8,128)(2,1)}, u32[]{:S(2)}, u32[]{:S(2)}) collective-permute-start(bf16[512,1280]{1,0:T(8,128)(2,1)} %dynamic-slice_bitcast_fusion.1), channel_id=1, source_target_pairs={{0,16},{16,0},{1,17},{17,1},{2,18},{18,2},{3,19},{19,3},{4,20},{20... | collective-permute-start | bytes 3932168 | tf_op jit(solution)/shard_map/ppermute | solution.py:28
  38.9 5.6 %collective-permute-start = (bf16[512,512]{1,0:T(8,128)(2,1)S(1)}, bf16[512,512]{1,0:T(8,128)(2,1)S(1)}, u32[]{:S(2)}, u32[]{:S(2)}) collective-permute-start(bf16[512,512]{1,0:T(8,128)(2,1)S(1)} %bitcast.47), channel_id=1, source_target_pairs={{0,16},{16,0},{1,17},{17,1},{2,18},{18,2},{3,19},{19,3},{4,20},{20... | collective-permute-start | bytes 1572872 | tf_op jit(solution)/shard_map/ppermute | solution.py:28
  43.2 1.2 collective-permute-start.1
  49.5 127.8 %all-gather.3.cloned.1.call-start = ((), (), s32[]{:S(2)}) async-start(), calls=%async_computation.6 | async-start | bytes 2949120 | tf_op jit(solution)/shard_map/all_gather | solution.py:74
  49.7 2.3 collective-permute-start.3
  123.0 154.5 %reduce-scatter.5.cloned.1.call-start = ((), (), s32[]{:S(2)}) async-start(), calls=%async_computation.7 | async-start | bytes 2949120 | tf_op jit(solution)/shard_map/reduce_scatter | solution.py:71
  125.5 3.4 collective-permute-start.4
  183.1 2.1 collective-permute-start.5
  186.6 16.3 %copy-start.11 = (bf16[1,512,2560]{2,1,0:T(8,128)(2,1)S(1)}, bf16[1,512,2560]{2,1,0:T(8,128)(2,1)}, u32[]{:S(2)}) copy-start(bf16[1,512,2560]{2,1,0:T(8,128)(2,1)} %param.7) | copy-start | bytes 7864324
  186.7 14.0 %collective-permute-start.6 = (bf16[512,512]{1,0:T(8,128)(2,1)S(1)}, bf16[512,512]{1,0:T(8,128)(2,1)S(1)}, u32[]{:S(2)}, u32[]{:S(2)}) collective-permute-start(bf16[512,512]{1,0:T(8,128)(2,1)S(1)} %add_convert_fusion.3), channel_id=1, source_target_pairs={{0,1},{1,0},{2,3},{3,2},{4,5},{5,4},{6,7},{7,6},{8,9},{9,8},{10,11... | collective-permute-start | bytes 1572872 | tf_op jit(solution)/shard_map/ppermute | solution.py:83
  200.9 2.0 collective-permute-start.7
  203.0 6.7 %copy-start.3 = (bf16[512,512]{1,0:T(8,128)(2,1)}, bf16[512,512]{1,0:T(8,128)(2,1)S(1)}, u32[]{:S(2)}) copy-start(bf16[512,512]{1,0:T(8,128)(2,1)S(1)} %get-tuple-element.6) | copy-start | bytes 1572868
  203.0 6.7 %copy-start.5 = (bf16[512,512]{1,0:T(8,128)(2,1)}, bf16[512,512]{1,0:T(8,128)(2,1)S(1)}, u32[]{:S(2)}) copy-start(bf16[512,512]{1,0:T(8,128)(2,1)S(1)} %get-tuple-element.7) | copy-start | bytes 1572868
  207.8 125.9 %all-gather.5.cloned.1.call-start = ((), (), s32[]{:S(2)}) async-start(), calls=%async_computation.8 | async-start | bytes 2949120 | tf_op jit(solution)/shard_map/all_gather | solution.py:74
  333.6 6.4 %copy-start.2 = (bf16[1024,1280]{1,0:T(8,128)(2,1)S(1)}, bf16[1024,1280]{1,0:T(8,128)(2,1)}, u32[]{:S(2)}) copy-start(bf16[1024,1280]{1,0:T(8,128)(2,1)} %all-gather.5.cloned.1.call-done) | copy-start | bytes 7864324
  340.0 8.9 %collective-permute-start.8 = (bf16[512,512]{1,0:T(8,128)(2,1)}, bf16[512,512]{1,0:T(8,128)(2,1)}, u32[]{:S(2)}, u32[]{:S(2)}) collective-permute-start(bf16[512,512]{1,0:T(8,128)(2,1)} %dynamic-slice_convert_fusion), channel_id=1, source_target_pairs={{0,16},{16,0},{1,17},{17,1},{2,18},{18,2},{3,19},{19,3},{4,20},{20... | collective-permute-start | bytes 1572872 | tf_op jit(solution)/shard_map/ppermute | solution.py:28
  341.9 40.0 %collective-permute-start.11 = (bf16[1024,1280]{1,0:T(8,128)(2,1)}, bf16[1024,1280]{1,0:T(8,128)(2,1)}, u32[]{:S(2)}, u32[]{:S(2)}) collective-permute-start(bf16[1024,1280]{1,0:T(8,128)(2,1)} %broadcast_select_fusion.2), channel_id=1, source_target_pairs={{0,16},{16,0},{1,17},{17,1},{2,18},{18,2},{3,19},{19,3},{4,20},{20... | collective-permute-start | bytes 7864328 | tf_op jit(solution)/shard_map/ppermute | solution.py:28
  344.7 30.5 %all-to-all-start.2 = ((bf16[128,8,512]{0,2,1:T(8,128)(2,1)}), bf16[128,8,512]{0,2,1:T(8,128)(2,1)}, u32[]{:S(2)}, u32[]{:S(2)}) async-start(bf16[128,8,512]{0,2,1:T(8,128)(2,1)} %bitcast.45), calls=%async_computation.4 | async-start | bytes 2097152 | tf_op jit(solution)/shard_map/all_to_all | solution.py:33
  350.6 13.9 %collective-permute-start.9 = (bf16[512,512]{1,0:T(8,128)(2,1)S(1)}, bf16[512,512]{1,0:T(8,128)(2,1)S(1)}, u32[]{:S(2)}, u32[]{:S(2)}) collective-permute-start(bf16[512,512]{1,0:T(8,128)(2,1)S(1)} %add_convert_fusion.1), channel_id=1, source_target_pairs={{0,1},{1,0},{2,3},{3,2},{4,5},{5,4},{6,7},{7,6},{8,9},{9,8},{10,11... | collective-permute-start | bytes 1572872 | tf_op jit(solution)/shard_map/ppermute | solution.py:83
  364.7 2.0 collective-permute-start.10
  375.1 29.8 %all-to-all-start.1 = ((bf16[8,128,512]{1,2,0:T(8,128)(2,1)}), bf16[8,128,512]{1,2,0:T(8,128)(2,1)}, u32[]{:S(2)}, u32[]{:S(2)}) async-start(bf16[8,128,512]{1,2,0:T(8,128)(2,1)} %copy.16), calls=%async_computation.3 | async-start | bytes 2097152 | tf_op jit(solution)/shard_map/all_to_all | solution.py:93
  (9 other events, 21.2 us)
Sparse Core Ops, SparseCore 0:
  49.6 71.2 reduce-scatter.2
  123.7 53.5 all-gather.2
  207.9 69.5 reduce-scatter.4
  280.1 53.4 all-gather.4
where the time goes:
time: 414 us; the launch traced here: 413 us
  waiting for transfers between devices  288 us (70%)
  blocking collectives  33.8 us (8%)
  local copies, waits for them, and re-layouts  22.6 us (5%)
  starting transfers between devices  20.3 us (5%)
  matrix products  20 us (5%)
  between operations  14.7 us (4%)
  other arithmetic  14.5 us (4%)
    reduce_scatter x2, waiting for transfers between devices, body(): pre = lax.psum_scatter(part, 'dp', scatter_dimension=0, tiled=True)  117 us
    all_gather x2, waiting for transfers between devices, body(): hidden_all = lax.all_gather(hidden, 'dp', axis=0, tiled=True)  103 us
    ppermute x2, waiting for transfers between devices, body(): got = lax.ppermute(sent, 'tensor', [(0, 1), (1, 0)])  24.6 us
    unnamed x1, blocking collectives  19.5 us
    all_to_all x1, waiting for transfers between devices, body(): lax.all_to_all(state_own, 'dp', split_axis=0, concat_axis=1, tiled=True)  16.5 us
    ppermute x10, waiting for transfers between devices, swap(): return lax.ppermute(array, 'section', [(0, 1), (1, 0)])  11.3 us
    all_to_all x1, waiting for transfers between devices, body(): lax.all_to_all(tok_full, 'dp', split_axis=1, concat_axis=0, tiled=True)  11.2 us
    all_gather x1, blocking collectives, body(): tok_full = lax.all_gather(tok_half, 'tensor', axis=1, tiled=True)  9.97 us
  transfers between devices with their start and end apart: 19, of which 15 were waited for; matrix products, arithmetic and copies ran while one was open for 6% of the time, Pallas kernels for 0%

commit v1 on v0

--- a/solution.py
+++ b/solution.py
@@ -90,7 +90,10 @@
         x = jnp.concatenate([new_a, new_b], axis=0)
         states.append(x)
     state_own = jnp.where(core == 0, states[0], states[1])
-    state_rows = lax.all_to_all(state_own, "dp", split_axis=0, concat_axis=1, tiled=True)
+    state_rows = jnp.concatenate(
+        lax.all_to_all(jnp.stack(jnp.split(state_own, lax.axis_size("dp"), axis=0)), "dp", 0, 0),
+        axis=1,
+    )
     state = lax.dynamic_slice_in_dim(state_rows, tensor_id * own_width, own_width, 1)
     hid_keep = jnp.where(core == 0, hiddens[0], hiddens[1])
     hid_got = swap(jnp.where(core == 0, hiddens[1], hiddens[0]))

time: 414 us -> 430 us (1.039)
  waiting for transfers between devices: 288 us -> 302 us
    all_to_all x1, waiting for transfers between devices: 4.83 us -> 19.1 us  [body(): lax.all_to_all(cotangent[0], 'dp', split_axis=1, concat_axis=0, tiled=True)]
    unnamed x30 -> x35, local copies, waits for them, and re-layouts: 8.5 us -> 11.9 us
where the time goes in v1:
time: 430 us; the launch traced here: 429 us
  waiting for transfers between devices  302 us (70%)
  blocking collectives  33.8 us (8%)
  local copies, waits for them, and re-layouts  24.3 us (6%)
  starting transfers between devices  20.3 us (5%)
  matrix products  19.8 us (5%)
  between operations  14.7 us (3%)
  other arithmetic  14.1 us (3%)
    reduce_scatter x2, waiting for transfers between devices, body(): pre = lax.psum_scatter(part, 'dp', scatter_dimension=0, tiled=True)  117 us
    all_gather x2, waiting for transfers between devices, body(): hidden_all = lax.all_gather(hidden, 'dp', axis=0, tiled=True)  103 us
    ppermute x2, waiting for transfers between devices, body(): got = lax.ppermute(sent, 'tensor', [(0, 1), (1, 0)])  24.7 us
    unnamed x1, blocking collectives  19.5 us
    all_to_all x1, waiting for transfers between devices, body(): lax.all_to_all(cotangent[0], 'dp', split_axis=1, concat_axis=0, tiled=True)  19.1 us
    all_to_all x1, waiting for transfers between devices, body(): lax.all_to_all(jnp.stack(jnp.split(state_own, lax.axis_size('dp'), axis=0...  16.4 us
    unnamed x35, local copies, waits for them, and re-layouts  11.9 us
    ppermute x10, waiting for transfers between devices, swap(): return lax.ppermute(array, 'section', [(0, 1), (1, 0)])  11.3 us
  transfers between devices with their start and end apart: 19, of which 15 were waited for; matrix products, arithmetic and copies ran while one was open for 6% of the time, Pallas kernels for 0%

profile of v1, /device:TPU:0, one launch (start us, length us, event | category | flops | bytes accessed | tf_op | source)
XLA Modules:
  0.0 429.0 jit_solution(96624576552657300)
XLA Ops:
  8.2 10.0 %all_gather.12 = bf16[64,4096]{1,0:T(8,128)(2,1)S(1)} all-gather(bf16[64,2048]{1,0:T(8,128)(2,1)S(1)} %constant_dynamic-slice_fusion.2), channel_id=1, replica_groups=mesh['section'=2,'dp'=8,'tensor'=2] {'tensor'}, dimensions={1}, use_global_device_ids=true | all-gather | bytes 786432 | tf_op jit(solution)/shard_map/all_gather | solution.py:36
  19.0 6.2 %all-to-all-start = ((bf16[64,8,512]{2,0,1:T(8,128)(2,1)}), bf16[64,8,512]{2,0,1:T(8,128)(2,1)S(1)}, u32[]{:S(2)}, u32[]{:S(2)}) async-start(bf16[64,8,512]{2,0,1:T(8,128)(2,1)} %bitcast.73), calls=%async_computation | async-start | bytes 1048576 | tf_op jit(solution)/shard_map/all_to_all | solution.py:41
  25.3 2.5 dynamic-slice_bitcast_fusion.1
  27.7 11.2 %all-to-all-done = bf16[64,8,512]{2,0,1:T(8,128)(2,1)S(1)} async-done(((bf16[64,8,512]{2,0,1:T(8,128)(2,1)}), bf16[64,8,512]{2,0,1:T(8,128)(2,1)S(1)}, u32[]{:S(2)}, u32[]{:S(2)}) %all-to-all-start) | async-done | bytes 524320 | tf_op jit(solution)/shard_map/all_to_all | solution.py:41
  38.9 4.3 %all_gather.13 = bf16[1,4096]{1,0:T(2,128)(2,1)S(1)} all-gather(bf16[1,2048]{1,0:T(2,128)(2,1)S(1)} %copy-done.11), channel_id=1, replica_groups=mesh['section'=2,'dp'=8,'tensor'=2] {'tensor'}, dimensions={1}, use_global_device_ids=true | all-gather | bytes 12288 | tf_op jit(solution)/shard_map/all_gather | solution.py:50
  46.4 3.1 convolution_convert_fusion.1
  52.2 68.8 %reduce-scatter.3.cloned.1.call-done = bf16[128,1280]{1,0:T(8,128)(2,1)} async-done(((bf16[1024,1280]{1,0:T(8,128)(2,1)}), bf16[128,1280]{1,0:T(8,128)(2,1)}) %reduce-scatter.3.cloned.1.call-update) | async-done | bytes 327696 | tf_op jit(solution)/shard_map/reduce_scatter | solution.py:71
  123.0 2.5 dynamic-slice_bitcast_fusion
  125.5 3.4 collective-permute-done.4
  128.9 48.4 %all-gather.3.cloned.1.call-done = bf16[1024,1280]{1,0:T(8,128)(2,1)} async-done(((bf16[128,1280]{1,0:T(8,128)(2,1)}), bf16[1024,1280]{1,0:T(8,128)(2,1)}) %all-gather.3.cloned.1.call-update) | async-done | bytes 2621456 | tf_op jit(solution)/shard_map/all_gather | solution.py:74
  177.3 3.7 fusion.10
  188.2 12.5 %collective-permute-done.6 = bf16[512,512]{1,0:T(8,128)(2,1)S(1)} collective-permute-done((bf16[512,512]{1,0:T(8,128)(2,1)S(1)}, bf16[512,512]{1,0:T(8,128)(2,1)S(1)}, u32[]{:S(2)}, u32[]{:S(2)}) %collective-permute-start.6) | collective-permute-done | bytes 524320 | tf_op jit(solution)/shard_map/ppermute | solution.py:83
  203.0 4.8 %convolution_convert_fusion = bf16[1024,1280]{1,0:T(8,128)(2,1)} fusion(bf16[512,1280]{1,0:T(8,128)(2,1)} %collective-permute-done.2, pred[]{:T(512)S(6)} %eq.2, bf16[1,512,2560]{2,1,0:T(8,128)(2,1)S(1)} %copy-done.10, s32[]{:T(128)S(6)} %select_n.141, f32[512]{0:T(512)S(1)} %bitcast.82, bf16[512,512]{1,0:T(8,128)(2,1)S(1)} %get-tuple-element.7, ...), kind=kOutput, calls=%fused_computation.6 | convolution fusion | flops 1347289088 | bytes 6293509 | tf_op jit(solution)/shard_map/dot_general | solution.py:70
  209.9 19.5 %all-reduce = f32[1024]{0:T(1024)S(1)} all-reduce(f32[1024]{0:T(1024)S(1)} %multiply_reduce_fusion), channel_id=4, replica_groups=mesh['section'=2,'dp'=8,'tensor'=2] {'dp'}, use_global_device_ids=true, to_apply=%region_4.5.clone | all-reduce | flops 1024 | bytes 8192
  229.5 48.0 %reduce-scatter.5.cloned.1.call-done = bf16[128,1280]{1,0:T(8,128)(2,1)} async-done(((bf16[1024,1280]{1,0:T(8,128)(2,1)}), bf16[128,1280]{1,0:T(8,128)(2,1)}) %reduce-scatter.5.cloned.1.call-update) | async-done | bytes 327696 | tf_op jit(solution)/shard_map/reduce_scatter | solution.py:71
  279.6 54.1 %all-gather.5.cloned.1.call-done = bf16[1024,1280]{1,0:T(8,128)(2,1)} async-done(((bf16[128,1280]{1,0:T(8,128)(2,1)}), bf16[1024,1280]{1,0:T(8,128)(2,1)}) %all-gather.5.cloned.1.call-update) | async-done | bytes 2621456 | tf_op jit(solution)/shard_map/all_gather | solution.py:74
  333.7 4.0 fusion.11
  341.8 12.2 %collective-permute-done.9 = bf16[512,512]{1,0:T(8,128)(2,1)S(1)} collective-permute-done((bf16[512,512]{1,0:T(8,128)(2,1)S(1)}, bf16[512,512]{1,0:T(8,128)(2,1)S(1)}, u32[]{:S(2)}, u32[]{:S(2)}) %collective-permute-start.9) | collective-permute-done | bytes 524320 | tf_op jit(solution)/shard_map/ppermute | solution.py:83
  359.6 4.3 all-to-all-start.2
  371.0 19.1 %all-to-all-done.2 = bf16[128,8,512]{0,2,1:T(8,128)(2,1)} async-done(((bf16[128,8,512]{0,2,1:T(8,128)(2,1)}), bf16[128,8,512]{0,2,1:T(8,128)(2,1)}, u32[]{:S(2)}, u32[]{:S(2)}) %all-to-all-start.2) | async-done | bytes 1048608 | tf_op jit(solution)/shard_map/all_to_all | solution.py:33
  390.1 4.4 %all-to-all-start.1 = ((bf16[8,128,512]{2,1,0:T(8,128)(2,1)}), bf16[8,128,512]{2,1,0:T(8,128)(2,1)}, u32[]{:S(2)}, u32[]{:S(2)}) async-start(bf16[8,128,512]{2,1,0:T(8,128)(2,1)} %fusion.39), calls=%async_computation.3 | async-start | bytes 2097152 | tf_op jit(solution)/shard_map/all_to_all | solution.py:94
  394.5 2.3 copy.19
  399.2 4.3 fusion.7
  403.4 16.4 %all-to-all-done.1 = bf16[8,128,512]{2,1,0:T(8,128)(2,1)} async-done(((bf16[8,128,512]{2,1,0:T(8,128)(2,1)}), bf16[8,128,512]{2,1,0:T(8,128)(2,1)}, u32[]{:S(2)}, u32[]{:S(2)}) %all-to-all-start.1) | async-done | bytes 1048608 | tf_op jit(solution)/shard_map/all_to_all | solution.py:94
  (94 shorter events, 44.5 us)
Async XLA Ops:
  19.0 19.8 %copy-start.11 = (bf16[1,2048]{1,0:T(2,128)(2,1)S(1)}, bf16[1,2048]{1,0:T(2,128)(2,1)}, u32[]{:S(2)}) copy-start(bf16[1,2048]{1,0:T(2,128)(2,1)} %param.6) | copy-start | bytes 12292
  19.0 19.8 %all-to-all-start = ((bf16[64,8,512]{2,0,1:T(8,128)(2,1)}), bf16[64,8,512]{2,0,1:T(8,128)(2,1)S(1)}, u32[]{:S(2)}, u32[]{:S(2)}) async-start(bf16[64,8,512]{2,0,1:T(8,128)(2,1)} %bitcast.73), calls=%async_computation | async-start | bytes 1048576 | tf_op jit(solution)/shard_map/all_to_all | solution.py:41
  25.2 95.7 %reduce-scatter.3.cloned.1.call-start = ((), (), s32[]{:S(2)}) async-start(), calls=%async_computation.5 | async-start | bytes 2949120 | tf_op jit(solution)/shard_map/reduce_scatter | solution.py:71
  27.7 17.3 %collective-permute-start.2 = (bf16[512,1280]{1,0:T(8,128)(2,1)}, bf16[512,1280]{1,0:T(8,128)(2,1)}, u32[]{:S(2)}, u32[]{:S(2)}) collective-permute-start(bf16[512,1280]{1,0:T(8,128)(2,1)} %dynamic-slice_bitcast_fusion.1), channel_id=1, source_target_pairs={{0,16},{16,0},{1,17},{17,1},{2,18},{18,2},{3,19},{19,3},{4,20},{20... | collective-permute-start | bytes 3932168 | tf_op jit(solution)/shard_map/ppermute | solution.py:28
  38.9 5.6 %collective-permute-start = (bf16[512,512]{1,0:T(8,128)(2,1)S(1)}, bf16[512,512]{1,0:T(8,128)(2,1)S(1)}, u32[]{:S(2)}, u32[]{:S(2)}) collective-permute-start(bf16[512,512]{1,0:T(8,128)(2,1)S(1)} %bitcast.77), channel_id=1, source_target_pairs={{0,16},{16,0},{1,17},{17,1},{2,18},{18,2},{3,19},{19,3},{4,20},{20... | collective-permute-start | bytes 1572872 | tf_op jit(solution)/shard_map/ppermute | solution.py:28
  43.2 1.2 collective-permute-start.1
  49.5 127.8 %all-gather.3.cloned.1.call-start = ((), (), s32[]{:S(2)}) async-start(), calls=%async_computation.6 | async-start | bytes 2949120 | tf_op jit(solution)/shard_map/all_gather | solution.py:74
  49.7 2.3 collective-permute-start.3
  123.0 154.5 %reduce-scatter.5.cloned.1.call-start = ((), (), s32[]{:S(2)}) async-start(), calls=%async_computation.7 | async-start | bytes 2949120 | tf_op jit(solution)/shard_map/reduce_scatter | solution.py:71
  125.5 3.4 collective-permute-start.4
  183.1 2.1 collective-permute-start.5
  186.6 16.3 %copy-start.10 = (bf16[1,512,2560]{2,1,0:T(8,128)(2,1)S(1)}, bf16[1,512,2560]{2,1,0:T(8,128)(2,1)}, u32[]{:S(2)}) copy-start(bf16[1,512,2560]{2,1,0:T(8,128)(2,1)} %param.7) | copy-start | bytes 7864324
  186.7 14.0 %collective-permute-start.6 = (bf16[512,512]{1,0:T(8,128)(2,1)S(1)}, bf16[512,512]{1,0:T(8,128)(2,1)S(1)}, u32[]{:S(2)}, u32[]{:S(2)}) collective-permute-start(bf16[512,512]{1,0:T(8,128)(2,1)S(1)} %add_convert_fusion.3), channel_id=1, source_target_pairs={{0,1},{1,0},{2,3},{3,2},{4,5},{5,4},{6,7},{7,6},{8,9},{9,8},{10,11... | collective-permute-start | bytes 1572872 | tf_op jit(solution)/shard_map/ppermute | solution.py:83
  200.9 2.0 collective-permute-start.7
  203.0 138.5 %copy-start.3 = (bf16[512,512]{1,0:T(8,128)(2,1)}, bf16[512,512]{1,0:T(8,128)(2,1)S(1)}, u32[]{:S(2)}) copy-start(bf16[512,512]{1,0:T(8,128)(2,1)S(1)} %get-tuple-element.6) | copy-start | bytes 1572868
  203.0 138.5 %copy-start.5 = (bf16[512,512]{1,0:T(8,128)(2,1)}, bf16[512,512]{1,0:T(8,128)(2,1)S(1)}, u32[]{:S(2)}) copy-start(bf16[512,512]{1,0:T(8,128)(2,1)S(1)} %get-tuple-element.7) | copy-start | bytes 1572868
  207.8 125.9 %all-gather.5.cloned.1.call-start = ((), (), s32[]{:S(2)}) async-start(), calls=%async_computation.8 | async-start | bytes 2949120 | tf_op jit(solution)/shard_map/all_gather | solution.py:74
  337.8 2.0 collective-permute-start.8
  340.0 14.0 %collective-permute-start.9 = (bf16[512,512]{1,0:T(8,128)(2,1)S(1)}, bf16[512,512]{1,0:T(8,128)(2,1)S(1)}, u32[]{:S(2)}, u32[]{:S(2)}) collective-permute-start(bf16[512,512]{1,0:T(8,128)(2,1)S(1)} %add_convert_fusion.1), channel_id=1, source_target_pairs={{0,1},{1,0},{2,3},{3,2},{4,5},{5,4},{6,7},{7,6},{8,9},{9,8},{10,11... | collective-permute-start | bytes 1572872 | tf_op jit(solution)/shard_map/ppermute | solution.py:83
  341.5 13.5 %copy-start.2 = (bf16[1024,1280]{1,0:T(8,128)(2,1)S(1)}, bf16[1024,1280]{1,0:T(8,128)(2,1)}, u32[]{:S(2)}) copy-start(bf16[1024,1280]{1,0:T(8,128)(2,1)} %all-gather.5.cloned.1.call-done) | copy-start | bytes 7864324
  355.0 8.9 %collective-permute-start.10 = (bf16[512,512]{1,0:T(8,128)(2,1)}, bf16[512,512]{1,0:T(8,128)(2,1)}, u32[]{:S(2)}, u32[]{:S(2)}) collective-permute-start(bf16[512,512]{1,0:T(8,128)(2,1)} %add_convert_fusion), channel_id=1, source_target_pairs={{0,16},{16,0},{1,17},{17,1},{2,18},{18,2},{3,19},{19,3},{4,20},{20... | collective-permute-start | bytes 1572872 | tf_op jit(solution)/shard_map/ppermute | solution.py:28
  356.8 40.0 %collective-permute-start.11 = (bf16[1024,1280]{1,0:T(8,128)(2,1)}, bf16[1024,1280]{1,0:T(8,128)(2,1)}, u32[]{:S(2)}, u32[]{:S(2)}) collective-permute-start(bf16[1024,1280]{1,0:T(8,128)(2,1)} %broadcast_select_fusion.2), channel_id=1, source_target_pairs={{0,16},{16,0},{1,17},{17,1},{2,18},{18,2},{3,19},{19,3},{4,20},{20... | collective-permute-start | bytes 7864328 | tf_op jit(solution)/shard_map/ppermute | solution.py:28
  359.6 30.5 %all-to-all-start.2 = ((bf16[128,8,512]{0,2,1:T(8,128)(2,1)}), bf16[128,8,512]{0,2,1:T(8,128)(2,1)}, u32[]{:S(2)}, u32[]{:S(2)}) async-start(bf16[128,8,512]{0,2,1:T(8,128)(2,1)} %bitcast.75), calls=%async_computation.4 | async-start | bytes 2097152 | tf_op jit(solution)/shard_map/all_to_all | solution.py:33
  390.1 29.8 %all-to-all-start.1 = ((bf16[8,128,512]{2,1,0:T(8,128)(2,1)}), bf16[8,128,512]{2,1,0:T(8,128)(2,1)}, u32[]{:S(2)}, u32[]{:S(2)}) async-start(bf16[8,128,512]{2,1,0:T(8,128)(2,1)} %fusion.39), calls=%async_computation.3 | async-start | bytes 2097152 | tf_op jit(solution)/shard_map/all_to_all | solution.py:94
  (8 other events, 23.2 us)
Sparse Core Ops, SparseCore 0:
  49.6 71.2 reduce-scatter.2
  123.7 53.5 all-gather.2
  207.9 69.5 reduce-scatter.4
  280.1 53.4 all-gather.4
